TPU v7x, 128 devices: a whole 4x4x4 slice. The times are simulated.
128 devices in a mesh: grp: 8 (over y, core), rep: 16 (over z, x).
Axes of the slice: x: 4, y: 4, z: 4, core: 2. Of those that a mesh axis runs over, the one named last changes fastest.
Arguments:
- coefficients: bfloat16 [16384, 2048], P(('grp', 'rep')), may hold values from -100 to 100
- truncation: int32 [16], replicated, may hold values from 16 to 64
- neighbours: int32 [50, 16384], P(None, ('grp', 'rep')), may hold values from 0 to 16383, as said below
- initial: float32 [32, 16384], P(None, ('grp', 'rep')), may hold values from -6 to 6
Outputs:
- alignment: float32 [2, 50, 16384], P(None, None, ('grp', 'rep'))
- vectors: float32 [32, 16384], P(None, ('grp', 'rep'))
Inputs may be any that keep to these rules, and one draw needn't show every extreme that they name: `neighbours`: every neighbour of a particle is another particle of the same block of 2048 particles that holds it (the particles of one group of 16 devices along rep). For each device, the neighbour slots of its 128 particles that name particles of one other device number at most 64; every device has, in every draw, one other device that its slots name exactly 64 times.
All inputs are finite; a program needn't handle non-finite values.
Results may differ from a plain program's by a relative error of at most 0.0003.
Values may be sent and summed in bfloat16 or wider, within the bound.
No kernel may reach another device: no remote copies, remote signals or barrier semaphores. Data moves between devices by JAX's collectives and lax.ppermute only.
A program may use at most 128 MiB of HBM per device.

v0:
```python
import functools

import jax
import jax.numpy as jnp
from jax import lax
from jax.experimental import pallas as pl
from jax.experimental.pallas import tpu as pltpu
from jax.sharding import Mesh
from jax.sharding import PartitionSpec as P

ANG = 64
RAD = 16
NB = 50
NBP = 56
VEC = 16
PD = 128
CAP = 64
CW = 2048
FULL = RAD * ANG
SIZES = (384, 512, 544, 576, 608, 640, 672, 704, 736, 768, 896, FULL)
HEAD = 2 * VEC
PEERS = 16
PAIRS = PEERS // 2
WIDE = 4
GROUP = 8
GRP = ("grp_0", "grp_1")
REP = ("rep_0", "rep_1")
GRP_REP = ("grp_0", "grp_1", "rep_0", "rep_1")
EPS = 1e-06
F32 = jnp.float32
BF16 = jnp.bfloat16
HIGHEST = lax.Precision.HIGHEST

NT = (((1,), (1,)), ((), ()))
TN = (((0,), (0,)), ((), ()))


def iota(shape, dim):
    return lax.broadcasted_iota(jnp.int32, shape, dim)


def one_hot(cond):
    return jnp.where(cond, 1.0, 0.0).astype(BF16)


def three_parts(x):
    high = x.astype(BF16)
    rest = x - high.astype(F32)
    mid = rest.astype(BF16)
    low = (rest - mid.astype(F32)).astype(BF16)
    return jnp.concatenate([high, mid, low], axis=0)


def two_parts(x):
    high = x.astype(BF16)
    rest = (x - high.astype(F32)).astype(BF16)
    return jnp.concatenate([high, rest], axis=0)


def exact_select(x, selector, dims=(((1,), (0,)), ((), ()))):
    rows = x.shape[0]
    parts = lax.dot_general(three_parts(x), selector, dims, preferred_element_type=F32)
    return parts[:rows] + (parts[rows : 2 * rows] + parts[2 * rows :])


def kept_rows(trunc_ref, rows, lanes):
    row = iota((rows, lanes), 0) % RAD
    kept = jnp.zeros((rows, lanes), jnp.int32)
    for q in range(RAD):
        kept = jnp.where(row == q, trunc_ref[q], kept)
    return kept


def place():
    index = [lax.axis_index(name) for name in GRP_REP]
    size = [lax.axis_size(name) for name in GRP_REP]
    group = index[0] * size[1] + index[1]
    member = index[2] * size[3] + index[3]
    return group * (size[2] * size[3] * PD), member


def slot_kernel(
    trunc_ref, nb_hbm, coef_hbm, init_hbm,
    which_ref, code_ref, lists_ref, names_ref, req_ref, coef_ref, init_ref,
    nb_ref, nbp_ref, a_ref, b_ref, sem_ref,
):
    bring = (
        pltpu.make_async_copy(coef_hbm, coef_ref, sem_ref.at[0]),
        pltpu.make_async_copy(init_hbm, init_ref, sem_ref.at[1]),
    )
    slots = pltpu.make_async_copy(nb_hbm, nb_ref, sem_ref.at[2])
    for copy in (slots,) + bring:
        copy.start()
    total = trunc_ref[0]
    for q in range(1, RAD):
        total = total + trunc_ref[q]
    which = jnp.int32(0)
    for size in SIZES[:-1]:
        which = which + (total > size).astype(jnp.int32)
    which_ref[0] = which
    start, me = place()
    slots.wait()
    nbp_ref[...] = jnp.full((NBP, PD), -1, jnp.int32)
    nbp_ref[:NB, :] = nb_ref[...] - start
    local = nbp_ref[...]
    owner = local >> 7
    within = local & (PD - 1)
    remote = (owner != me) & (local >= 0)
    owner = jnp.where(remote, owner, -1)
    masks = [one_hot(owner == p) for p in range(PEERS)]
    before = one_hot(iota((NBP, NBP), 0) > iota((NBP, NBP), 1))
    in_column = jnp.dot(before, jnp.concatenate(masks, axis=1), preferred_element_type=F32)
    totals = jnp.concatenate(
        [jnp.sum(m.astype(F32), axis=0, keepdims=True) for m in masks], axis=0
    )
    left = one_hot(iota((PD, PD), 0) < iota((PD, PD), 1))
    columns = jnp.dot(totals.astype(BF16), left, preferred_element_type=F32)
    rank = jnp.zeros((NBP, PD), F32)
    for p in range(PEERS):
        here = in_column[:, p * PD : (p + 1) * PD] + columns[p : p + 1, :]
        rank = jnp.where(owner == p, here, rank)
    rank = rank.astype(jnp.int32)
    code = jnp.where(remote, owner * CAP + rank, -1)
    pair = code >> 7
    lane = jnp.where(remote, code & (PD - 1), -1)
    particle = iota((1, PD), 1).astype(F32) + 1.0
    rows8 = iota((PAIRS, PD), 0)
    rows128 = iota((PD, PD), 0)
    for n in range(NB):
        mine = rows8 == pair[n : n + 1, :]
        names = within[n : n + 1, :].astype(F32)
        both = jnp.concatenate(
            [jnp.where(mine, names, 0.0), jnp.where(mine, particle, 0.0)], axis=0
        )
        a_ref[:, n * PD : (n + 1) * PD] = both.astype(BF16)
        b_ref[:, n * PD : (n + 1) * PD] = one_hot(rows128 == lane[n : n + 1, :])
    lists = lax.dot_general(a_ref[...], b_ref[...], NT, preferred_element_type=F32)
    turned = pltpu.roll(lists, CAP, 1)
    first = iota((2 * PAIRS, PD), 1) < CAP
    both = (jnp.where(first, lists, turned), jnp.where(first, turned, lists))
    for p in range(PEERS):
        r = p // 2
        req_ref[p] = both[p % 2][r : r + 1, :]
    lists_ref[...] = lists[PAIRS:]
    code_ref[...] = code
    for p in range(PEERS):
        r = p // 2
        names_ref[p : p + 1, :] = both[p % 2][PAIRS + r : PAIRS + r + 1, :]
    for copy in bring:
        copy.wait()


def wanted_row(rx_ref, r):
    even = rx_ref[2 * r]
    odd = rx_ref[2 * r + 1]
    return jnp.where(iota((1, PD), 1) < CAP, even, odd).astype(jnp.int32)


def local_kernel(
    trunc_ref, coef_ref, init_ref, out_ref, e_ref, re_ref, im_ref,
    f_ref, wide_re_ref, wide_im_ref, s_ref,
):
    init = init_ref[...]
    parts = two_parts(jnp.concatenate([init[:VEC], init[VEC:]], axis=1))
    out_ref[:HEAD, :] = parts
    for c in range(CW // PD):
        block = coef_ref[:, c * PD : (c + 1) * PD].astype(F32)
        f_ref[c * PD : (c + 1) * PD, :] = block.T
    offset = 0
    for q in range(RAD):
        here = pl.ds(offset, ANG)
        wide_re_ref[here, :] = f_ref[q * ANG : (q + 1) * ANG, :]
        wide_im_ref[here, :] = f_ref[(RAD + q) * ANG : (RAD + q + 1) * ANG, :]
        offset = offset + trunc_ref[q]
    for b in range(FULL // PD):
        rows = slice(b * PD, (b + 1) * PD)
        to = slice(HEAD + b * PD, HEAD + (b + 1) * PD)
        kept = iota((PD, PD), 0) + b * PD < offset
        out_ref[to, :PD] = jnp.where(kept, wide_re_ref[rows, :], 0.0).astype(BF16)
        out_ref[to, PD:] = jnp.where(kept, wide_im_ref[rows, :], 0.0).astype(BF16)
    own_pairs(trunc_ref, e_ref, re_ref, im_ref, f_ref, s_ref)


def pick_kernel(size, rx_ref, pack_ref, out_ref):
    rows = iota((PD, PD), 0)
    first = iota((PD, PD), 1) < CAP

    def step(r, carry):
        sides = []
        for p in range(WIDE):
            picked = rows == rx_ref[WIDE * r + p].astype(jnp.int32)
            top = one_hot(picked & first)
            bottom = one_hot(picked & jnp.logical_not(first))
            sides.append(jnp.concatenate([top, bottom], axis=0))
        side = jnp.concatenate(sides, axis=1)
        chosen = jnp.dot(pack_ref[:size, :], side, preferred_element_type=F32)
        for p in range(WIDE):
            out_ref[WIDE * r + p] = chosen[:, p * PD : (p + 1) * PD].astype(BF16)
        return carry

    lax.fori_loop(0, PEERS // WIDE, step, 0)


def own_pairs(trunc_ref, e_ref, re_ref, im_ref, xt_ref, s_ref):
    kept = kept_rows(trunc_ref, 2 * RAD, PD)
    e_ref[...] = jnp.zeros((PD, PD), F32)
    re_ref[...] = jnp.zeros((PD, PD), F32)
    im_ref[...] = jnp.zeros((PD, PD), F32)

    def sums(first):
        for b in range(PD // 8):
            sub = slice(b * 8, (b + 1) * 8)
            energy = e_ref[sub, :]
            m_re = re_ref[sub, :]
            m_im = im_ref[sub, :]
            before = max(first - 1, 0)
            re = s_ref[before, sub, :PD]
            im = s_ref[before, sub, PD:]
            for k in range(first, first + GROUP):
                if k == 0:
                    energy = energy + re * re
                    continue
                next_re = s_ref[k, sub, :PD]
                next_im = s_ref[k, sub, PD:]
                half_re = 0.5 * next_re
                half_im = 0.5 * next_im
                energy = energy + (half_re * next_re + half_im * next_im)
                if k == 1:
                    m_re = m_re + re * next_re
                    m_im = m_im - re * next_im
                else:
                    m_re = m_re + (re * half_re + im * half_im)
                    m_im = m_im + (im * half_re - re * half_im)
                re, im = next_re, next_im
            e_ref[sub, :] = energy
            re_ref[sub, :] = m_re
            im_ref[sub, :] = m_im

    for first in range(0, ANG, GROUP):
        for k in range(first, first + GROUP):
            rows = xt_ref[pl.ds(k, 2 * RAD, stride=ANG), :]
            masked = rows if k < 16 else jnp.where(kept > k, rows, 0.0)
            turned = jnp.concatenate([masked[RAD:], -masked[:RAD]], axis=0)
            right = jnp.concatenate([masked, turned], axis=1).astype(BF16)
            s_ref[k] = lax.dot_general(
                rows.astype(BF16), right, TN, preferred_element_type=F32
            )
        if first > 0:
            sums(first - GROUP)
    sums(ANG - GROUP)


def far_kernel(
    size, trunc_ref, names_ref, pack_ref, recv_ref, table_ref, cur_ref,
    same_ref, cross_ref,
):
    kept = size - HEAD
    for b in range(WIDE // 2):
        same_ref[b, kept:, :] = jnp.zeros((ANG, PD), F32)
        cross_ref[b, kept:, :] = jnp.zeros((ANG, PD), F32)

    def step(r, carry):
        far_step(
            size, r, trunc_ref, names_ref, pack_ref, recv_ref, table_ref, cur_ref,
            same_ref, cross_ref,
        )
        return carry

    lax.fori_loop(0, PEERS // WIDE, step, 0)


def far_step(
    size, r, trunc_ref, names_ref, pack_ref, recv_ref, table_ref, cur_ref,
    same_ref, cross_ref,
):
    kept = size - HEAD
    first = iota((1, PD), 1) < CAP
    picks = []
    for b in range(WIDE // 2):
        even = names_ref[pl.ds(WIDE * r + 2 * b, 1), :]
        odd = names_ref[pl.ds(WIDE * r + 2 * b + 1, 1), :]
        name = jnp.where(first, even, odd).astype(jnp.int32)
        picks.append(one_hot(iota((PD, PD), 0) + 1 == name))
    pick = jnp.concatenate(picks, axis=1)
    mine_re = jnp.dot(pack_ref[HEAD:size, :PD], pick, preferred_element_type=F32)
    mine_im = jnp.dot(pack_ref[HEAD:size, PD:], pick, preferred_element_type=F32)
    for p in range(WIDE):
        parts = recv_ref[WIDE * r + p, :HEAD, :].astype(F32)
        cur_ref[WIDE * r + p] = parts[:VEC] + parts[VEC:]
    for b in range(WIDE // 2):
        even = recv_ref[WIDE * r + 2 * b, HEAD:, :].astype(F32)
        odd = recv_ref[WIDE * r + 2 * b + 1, HEAD:, :].astype(F32)
        b_re = jnp.where(first, even, pltpu.roll(odd, CAP, 1))
        b_im = jnp.where(first, pltpu.roll(even, CAP, 1), odd)
        a_re = mine_re[:, b * PD : (b + 1) * PD]
        a_im = mine_im[:, b * PD : (b + 1) * PD]
        same_ref[b, :kept, :] = a_re * b_re + a_im * b_im
        cross_ref[b, :kept, :] = a_im * b_re - a_re * b_im
    freq = iota((ANG, PD), 0)
    totals = [[jnp.zeros((ANG, PD), F32)] * 2 for _ in range(WIDE // 2)]
    offset = 0
    for q in range(RAD):
        here = pl.ds(offset, ANG)
        inside = freq < trunc_ref[q]
        for b in range(WIDE // 2):
            for v, ref in enumerate((same_ref, cross_ref)):
                totals[b][v] = totals[b][v] + jnp.where(inside, ref[b, here, :], 0.0)
        offset = offset + trunc_ref[q]
    inner = (freq > 0) & (freq < ANG - 1)
    for b in range(WIDE // 2):
        s_re, s_im = totals[b]
        power = s_re * s_re + s_im * s_im
        next_re = pltpu.roll(s_re, ANG - 1, 0)
        next_im = pltpu.roll(s_im, ANG - 1, 0)
        zero_re = s_re[:1]
        energy = zero_re * zero_re + 0.5 * jnp.sum(
            jnp.where(freq == 0, 0.0, power), axis=0, keepdims=True
        )
        m_re = zero_re * s_re[1:2] + 0.5 * jnp.sum(
            jnp.where(inner, s_re * next_re + s_im * next_im, 0.0), axis=0, keepdims=True
        )
        m_im = 0.5 * jnp.sum(
            jnp.where(inner, s_im * next_re - s_re * next_im, 0.0), axis=0, keepdims=True
        ) - zero_re * s_im[1:2]
        table_ref[WIDE // 2 * r + b] = jnp.concatenate(
            [energy, m_re, m_im, jnp.zeros((5, PD), F32)], axis=0
        )


def near_image(cur, w_re, w_im):
    weights = jnp.concatenate([w_re, w_im], axis=1)
    both = jnp.dot(cur, weights, precision=HIGHEST, preferred_element_type=F32)
    re = both[:VEC, :PD] - both[VEC:, PD:]
    im = both[VEC:, :PD] + both[:VEC, PD:]
    return jnp.concatenate([re, im], axis=0)


def far_image(slots, table_ref, lists_ref):
    values = []
    picks = []
    for r in range(PAIRS):
        m_re = table_ref[r, 1:2, :]
        m_im = table_ref[r, 2:3, :]
        c_re, c_im = slots[r][:VEC], slots[r][VEC:]
        values.append(
            jnp.concatenate([m_re * c_re - m_im * c_im, m_re * c_im + m_im * c_re], axis=0)
        )
        particle = lists_ref[r : r + 1, :].astype(jnp.int32)
        picks.append(one_hot(iota((PD, PD), 0) + 1 == particle))
    return exact_select(
        jnp.concatenate(values, axis=1), jnp.concatenate(picks, axis=1), NT
    )


def send_columns(cur, rx_ref, out_ref):
    picks = [one_hot(iota((PD, PD), 0) == wanted_row(rx_ref, r)) for r in range(PAIRS)]
    columns = exact_select(cur, jnp.concatenate(picks, axis=1))
    first = iota((VEC, PD), 1) < CAP
    for r in range(PAIRS):
        re = columns[:VEC, r * PD : (r + 1) * PD]
        im = columns[VEC:, r * PD : (r + 1) * PD]
        out_ref[2 * r] = jnp.where(first, re, pltpu.roll(im, CAP, 1))
        out_ref[2 * r + 1] = jnp.where(first, pltpu.roll(re, CAP, 1), im)


def received_columns(recv_ref):
    first = iota((VEC, PD), 1) < CAP
    slots = []
    for r in range(PAIRS):
        even = recv_ref[2 * r]
        odd = recv_ref[2 * r + 1]
        re = jnp.where(first, even, pltpu.roll(odd, CAP, 1))
        im = jnp.where(first, pltpu.roll(even, CAP, 1), odd)
        slots.append(jnp.concatenate([re, im], axis=0))
    return slots


def first_kernel(
    nb_ref, code_ref, lists_ref, table_ref, e_ref, re_ref, im_ref,
    slots_ref, init_ref, rx_ref,
    align_hbm, weights_ref, degree_ref, cur_ref, send_ref,
    near_ref, align_ref, sem_ref,
):
    start, me = place()
    local = nb_ref[...] - start
    near = (local >> 7) == me
    near_ref[...] = jnp.full((PD, PD), -1.0, F32)
    near_ref[:NB, :] = jnp.where(near, local & (PD - 1), -1).astype(F32)
    rows = iota((PD, PD), 0).astype(F32)
    counts = jnp.zeros((PD, PD), F32)
    for n in range(NB):
        counts = counts + jnp.where(rows == near_ref[n : n + 1, :], 1.0, 0.0)
    named = near_ref[...].T.astype(jnp.int32)
    inside = jnp.maximum(named, 0)
    values = []
    for ref, sign in ((e_ref, 1.0), (re_ref, 1.0), (im_ref, -1.0)):
        found = jnp.take_along_axis(ref[...], inside, axis=1, mode="promise_in_bounds")
        values.append(jnp.where(named >= 0, sign * found, 0.0).T[:NBP])
    code = code_ref[...]
    pair = code >> 7
    lane = code & (PD - 1)
    for r in range(PAIRS):
        mine = pair == r
        for v in range(3):
            row = jnp.broadcast_to(table_ref[r, v : v + 1, :], (NBP, PD))
            found = jnp.take_along_axis(row, lane, axis=1, mode="promise_in_bounds")
            values[v] = jnp.where(mine, found, values[v])
    below = values[0] + EPS
    align_ref[:, 0, :] = (values[1] / below)[:NB]
    align_ref[:, 1, :] = (values[2] / below)[:NB]
    leaving = pltpu.make_async_copy(align_ref, align_hbm, sem_ref.at[0])
    leaving.start()
    degree = EPS + jnp.sum(values[0], axis=0, keepdims=True)
    degree_ref[...] = jnp.broadcast_to(degree, (8, PD))
    w_re = counts * re_ref[...]
    w_im = counts * im_ref[...]
    weights_ref[0] = w_re
    weights_ref[1] = w_im
    slots = received_columns(slots_ref)
    image = near_image(init_ref[...], w_re, w_im) + far_image(slots, table_ref, lists_ref)
    image = image / degree
    cur_ref[...] = image
    send_columns(image, rx_ref, send_ref)
    leaving.wait()


def next_image(recv_ref, cur_ref, weights_ref, degree_ref, table_ref, lists_ref):
    slots = received_columns(recv_ref)
    image = near_image(cur_ref[...], weights_ref[0], weights_ref[1])
    image = image + far_image(slots, table_ref, lists_ref)
    return image / degree_ref[:1, :]


def middle_kernel(
    recv_ref, cur_ref, weights_ref, degree_ref, table_ref, lists_ref, rx_ref,
    out_ref, send_ref,
):
    image = next_image(recv_ref, cur_ref, weights_ref, degree_ref, table_ref, lists_ref)
    out_ref[...] = image
    send_columns(image, rx_ref, send_ref)


def last_kernel(
    total, recv_ref, cur_ref, weights_ref, degree_ref, table_ref, lists_ref,
    out_ref, gram_ref,
):
    image = next_image(recv_ref, cur_ref, weights_ref, degree_ref, table_ref, lists_ref)
    out_ref[...] = image
    gram = lax.dot_general(
        image[:VEC], image[:VEC], NT, precision=HIGHEST, preferred_element_type=F32
    ) + lax.dot_general(
        image[VEC:], image[VEC:], NT, precision=HIGHEST, preferred_element_type=F32
    )
    gram = gram * (1.0 / total)
    wide = jnp.concatenate([gram] * 8, axis=1)
    mine = iota((VEC, PD), 1) // VEC == iota((VEC, PD), 0) % 8
    wide = jnp.where(mine, wide, 0.0)
    packed = jnp.concatenate(
        [
            jnp.sum(wide[:8], axis=0, keepdims=True),
            jnp.sum(wide[8:], axis=0, keepdims=True),
        ],
        axis=0,
    )
    gram_ref[...] = jnp.broadcast_to(packed[None], gram_ref.shape)


def finish_kernel(grams_ref, cur_ref, out_ref):
    packed = jnp.sum(grams_ref[...], axis=0)
    row = iota((VEC, PD), 0)
    lane = iota((VEC, PD), 1)
    wide = jnp.where(row < 8, packed[0:1, :], packed[1:2, :])
    wide = jnp.where(lane // VEC == row % 8, wide, 0.0)
    for shift in (64, 32, 16):
        wide = wide + pltpu.roll(wide, shift, 1)
    columns = [jnp.broadcast_to(wide[:, c : c + 1], (VEC, PD)) for c in range(VEC)]
    re = cur_ref[:VEC, :]
    im = cur_ref[VEC:, :]
    for c in range(VEC):
        pivot = columns[c][c : c + 1, :]
        scale = lax.rsqrt(pivot)
        scale = scale * (1.5 - 0.5 * pivot * scale * scale)
        column = jnp.where(row > c, columns[c] * scale, 0.0)
        for d in range(c + 1, VEC):
            columns[d] = columns[d] - column * (columns[d][c : c + 1, :] * scale)
        top_re = re[c : c + 1, :] * scale
        top_im = im[c : c + 1, :] * scale
        here = row == c
        re = jnp.where(here, top_re, re - column * top_re)
        im = jnp.where(here, top_im, im - column * top_im)
    out_ref[:VEC, :] = re
    out_ref[VEC:, :] = im


def struct(shape, dtype=F32):
    return jax.ShapeDtypeStruct(shape, dtype)


SMEM = pl.BlockSpec(memory_space=pltpu.SMEM)
VMEM = pl.BlockSpec(memory_space=pltpu.VMEM)
HBM = pl.BlockSpec(memory_space=pltpu.HBM)


def grant(mib):
    return pltpu.CompilerParams(vmem_limit_bytes=mib << 20)


def exchange(size, truncation, names, asked, packed):
    sent = pl.pallas_call(
        functools.partial(pick_kernel, size),
        out_shape=struct((PEERS, size, PD), BF16),
        in_specs=[VMEM, VMEM],
        out_specs=VMEM,
        compiler_params=grant(16),
        name="pick",
    )(asked, packed)
    received = lax.all_to_all(sent, REP, 0, 0, tiled=True)
    return pl.pallas_call(
        functools.partial(far_kernel, size),
        out_shape=(struct((PAIRS, 8, PD)), struct((PEERS, VEC, PD))),
        in_specs=[SMEM, VMEM, VMEM, VMEM],
        out_specs=(VMEM, VMEM),
        scratch_shapes=[
            pltpu.VMEM((WIDE // 2, size - HEAD + ANG, PD), F32),
            pltpu.VMEM((WIDE // 2, size - HEAD + ANG, PD), F32),
        ],
        compiler_params=grant(20),
        name="far",
    )(truncation, names, packed, received)


def shards(coefficients, truncation, neighbours, initial):
    groups = lax.axis_size(GRP)
    replicas = lax.axis_size(REP)
    devices = groups * replicas
    which, code, lists, names, requests, coefficients, initial = pl.pallas_call(
        slot_kernel,
        out_shape=(
            struct((1,), jnp.int32),
            struct((NBP, PD), jnp.int32),
            struct((PAIRS, PD)),
            struct((PEERS, PD)),
            struct((PEERS, 1, PD)),
            struct((PD, CW), BF16),
            struct((32, PD)),
        ),
        in_specs=[SMEM, HBM, HBM, HBM],
        out_specs=(SMEM,) + (VMEM,) * 6,
        compiler_params=grant(6),
        scratch_shapes=[
            pltpu.VMEM((NB, PD), jnp.int32),
            pltpu.VMEM((NBP, PD), jnp.int32),
            pltpu.VMEM((2 * PAIRS, NB * PD), BF16),
            pltpu.VMEM((PD, NB * PD), BF16),
            pltpu.SemaphoreType.DMA((3,)),
        ],
        name="slots",
    )(
        truncation,
        *(
            pltpu.with_memory_space_constraint(x, pltpu.HBM)
            for x in (neighbours, coefficients, initial)
        ),
    )
    asked = lax.all_to_all(requests, REP, 0, 0, tiled=True)
    packed, e_own, re_own, im_own = pl.pallas_call(
        local_kernel,
        out_shape=(struct((HEAD + FULL, 2 * PD), BF16),) + (struct((PD, PD)),) * 3,
        in_specs=[SMEM, VMEM, VMEM],
        scratch_shapes=[
            pltpu.VMEM((CW, PD), F32),
            pltpu.VMEM((FULL + ANG, PD), F32),
            pltpu.VMEM((FULL + ANG, PD), F32),
            pltpu.VMEM((ANG, PD, 2 * PD), F32),
        ],
        cost_estimate=pl.CostEstimate(
            flops=20_000_000_000, bytes_accessed=1_000_000, transcendentals=0
        ),
        compiler_params=grant(20),
        name="local",
    )(truncation, coefficients, initial)
    table, slots = lax.switch(
        which[0],
        [functools.partial(exchange, HEAD + size) for size in SIZES],
        truncation, names, asked, packed,
    )
    alignment, weights, degree, current, columns = pl.pallas_call(
        first_kernel,
        out_shape=(
            struct((NB, 2, PD)),
            struct((2, PD, PD)),
            struct((8, PD)),
            struct((32, PD)),
            struct((PEERS, VEC, PD)),
        ),
        in_specs=[VMEM] * 10,
        compiler_params=grant(6),
        out_specs=(HBM, VMEM, VMEM, VMEM, VMEM),
        scratch_shapes=[
            pltpu.VMEM((PD, PD), F32),
            pltpu.VMEM((NB, 2, PD), F32),
            pltpu.SemaphoreType.DMA((1,)),
        ],
        name="first",
    )(
        neighbours, code, lists, table, e_own, re_own, im_own,
        slots, initial, asked,
    )
    columns = lax.all_to_all(columns, REP, 0, 0, tiled=True)
    current, columns = pl.pallas_call(
        middle_kernel,
        out_shape=(struct((32, PD)), struct((PEERS, VEC, PD))),
        compiler_params=grant(6),
        name="middle",
    )(columns, current, weights, degree, table, lists, asked)
    columns = lax.all_to_all(columns, REP, 0, 0, tiled=True)
    current, gram = pl.pallas_call(
        functools.partial(last_kernel, float(PD * devices)),
        out_shape=(struct((32, PD)), struct((devices, 2, PD))),
        compiler_params=grant(6),
        name="last",
    )(columns, current, weights, degree, table, lists)
    grams = lax.all_to_all(gram, GRP_REP, 0, 0, tiled=True)
    vectors = pl.pallas_call(
        finish_kernel,
        out_shape=struct((32, PD)),
        compiler_params=grant(6),
        name="finish",
    )(grams, current)
    return (jnp.transpose(alignment, (1, 0, 2)), vectors)


def solution(mesh):
    split = Mesh(mesh.devices.reshape(4, 2, 4, 4), GRP_REP)
    in_specs = (P(GRP_REP, None), P(), P(None, GRP_REP), P(None, GRP_REP))
    out_specs = (P(None, None, GRP_REP), P(None, GRP_REP))
    return jax.shard_map(
        shards, mesh=split, in_specs=in_specs, out_specs=out_specs, check_vma=False
    )
```

profile of v0, /device:TPU:1, one launch (start us, length us, event | category | flops | bytes accessed | tf_op | source)
XLA Modules:
  0.0 103.5 jit_solution(3100039498033952907)
XLA Ops:
  0.6 3.1 %slots.1 = (s32[1]{0:T(128)}, s32[56,128]{1,0:T(8,128)S(1)}, f32[8,128]{1,0:T(8,128)S(1)}, f32[16,128]{1,0:T(8,128)S(1)}, f32[16,1,128]{2,1,0:T(1,128)}, /*index...) custom-call(s32[16]{0:T(128)} %trunc_ref.3, s32[50,128]{1,0:T(8,128)} %nb_ref.1, bf16[128,2048]{1,0:T(8,128)(2,1)} %coef_hbm.1, ...), custom_call_target="tpu_custom_call" | custom-call | tf_op jit(solution)/shard_map/slots/pallas_call | solution.py:536
  3.7 8.4 %all-to-all-start.12 = ((f32[16,1,128]{2,1,0:T(1,128)}), f32[16,1,128]{2,1,0:T(1,128)S(1)}, u32[]{:S(2)}, u32[]{:S(2)}) async-start(f32[16,1,128]{2,1,0:T(1,128)} %get-tuple-element.171), calls=%async_computation.12 | async-start | bytes 16384 | tf_op jit(solution)/shard_map/all_to_all | solution.py:565
  12.2 0.0 copy-start.1
  12.2 4.1 %local.1 = (bf16[1056,256]{1,0:T(8,128)(2,1)S(1)}, f32[128,128]{1,0:T(8,128)S(1)}, f32[128,128]{1,0:T(8,128)S(1)}, f32[128,128]{1,0:T(8,128)S(1)}) custom-call(s32[16]{0:T(128)} %trunc_ref.3, bf16[128,2048]{1,0:T(8,128)(2,1)S(1)} %get-tuple-element.172.coef_ref, f32[32,128]{1,0:T(8,128)S(1)} %get-tuple-element.173.init_ref), custom_call_target="tpu_custom_call" | custom-call | flops 20000000000 | bytes 1000000 | tf_op jit(solution)/shard_map/local/pallas_call | solution.py:566
  16.9 1.6 %all-to-all-done.12.rx_ref = f32[16,1,128]{2,1,0:T(1,128)S(1)} async-done(((f32[16,1,128]{2,1,0:T(1,128)}), f32[16,1,128]{2,1,0:T(1,128)S(1)}, u32[]{:S(2)}, u32[]{:S(2)}) %all-to-all-start.12) | async-done | bytes 8224 | tf_op jit(solution)/shard_map/all_to_all | solution.py:565
  18.5 0.0 copy-done.1
  18.5 0.0 copy-start
  18.5 41.0 %conditional.1 = ((f32[8,8,128]{2,1,0:T(8,128)S(1)}, f32[16,16,128]{2,1,0:T(8,128)S(1)})) conditional(s32[]{:T(128)} %bitcast, (f32[16,1,128]{2,1,0:T(1,128)S(1)}, bf16[1056,256]{1,0:T(8,128)(2,1)S(1)}, s32[16]{0:T(128)S(1)}, f32[16,128]{1,0:T(8,128)S(1)}) %tuple.70, (f32[16,1,128]{2,1,0:T(1,128)S(1)}, ...), branch_computations={%region_0.0_spmd, %region_1.0_spmd, %region_2.0_spmd, %region_3.0_... | conditional | bytes 8650760 | solution.py:582
  18.5 1.4 %pick.15 = bf16[16,608,128]{2,1,0:T(8,128)(2,1)S(1)} custom-call(f32[16,1,128]{2,1,0:T(1,128)S(1)} %get-tuple-element.111.rx_ref, bf16[1056,256]{1,0:T(8,128)(2,1)S(1)} %get-tuple-element.110.pack_ref), custom_call_target="tpu_custom_call" | custom-call | tf_op jit(solution)/shard_map/cond/branch_3_fun/pick/pallas_call | solution.py:509
  19.9 36.3 %all_to_all.71.recv_ref = bf16[16,608,128]{2,1,0:T(8,128)(2,1)S(1)} all-to-all(bf16[16,608,128]{2,1,0:T(8,128)(2,1)S(1)} %pick.15), channel_id=1, replica_groups=mesh['grp_0'=4,'grp_1'=2,'rep_0'=4,'rep_1'=4] {'rep_0','rep_1'}, dimensions={0} | all-to-all | bytes 4980736 | tf_op jit(solution)/shard_map/cond/branch_3_fun/all_to_all | solution.py:517
  56.2 3.1 %far.15 = (f32[8,8,128]{2,1,0:T(8,128)S(1)}, f32[16,16,128]{2,1,0:T(8,128)S(1)}) custom-call(s32[16]{0:T(128)S(1)} %get-tuple-element.108.trunc_ref, f32[16,128]{1,0:T(8,128)S(1)} %get-tuple-element.109.names_ref, bf16[1056,256]{1,0:T(8,128)(2,1)S(1)} %get-tuple-element.110.pack_ref, bf16[16,608,128]{2,1,0:T(8,128)(2,1)S(1)} %all_to_all.71.recv_ref), custom_call_target="tpu_custom_call" | custom-call | tf_op jit(solution)/shard_map/cond/branch_3_fun/far/pallas_call | solution.py:518
  59.5 0.0 copy-done
  59.6 1.7 %first.1 = (f32[50,2,128]{2,1,0:T(2,128)}, f32[2,128,128]{2,1,0:T(8,128)S(1)}, f32[8,128]{1,0:T(8,128)S(1)}, f32[32,128]{1,0:T(8,128)S(1)}, f32[16,16,128]{2,1,0:T(8,128)S(1)}) custom-call(s32[50,128]{1,0:T(8,128)S(1)} %copy-done, s32[56,128]{1,0:T(8,128)S(1)} %get-tuple-element.168.code_ref, f32[8,128]{1,0:T(8,128)S(1)} %get-tuple-element.169.lists_ref, ...), custom_call_target="tpu_custom_call" | custom-call | tf_op jit(solution)/shard_map/first/pallas_call | solution.py:587
  61.3 9.5 %all_to_all.80.recv_ref = f32[16,16,128]{2,1,0:T(8,128)S(1)} all-to-all(f32[16,16,128]{2,1,0:T(8,128)S(1)} %get-tuple-element.182), channel_id=1, replica_groups=mesh['grp_0'=4,'grp_1'=2,'rep_0'=4,'rep_1'=4] {'rep_0','rep_1'}, dimensions={0} | all-to-all | bytes 262144 | tf_op jit(solution)/shard_map/all_to_all | solution.py:609
  70.8 0.6 middle.1
  71.3 9.9 %all_to_all.81.recv_ref = f32[16,16,128]{2,1,0:T(8,128)S(1)} all-to-all(f32[16,16,128]{2,1,0:T(8,128)S(1)} %get-tuple-element.186), channel_id=1, replica_groups=mesh['grp_0'=4,'grp_1'=2,'rep_0'=4,'rep_1'=4] {'rep_0','rep_1'}, dimensions={0} | all-to-all | bytes 262144 | tf_op jit(solution)/shard_map/all_to_all | solution.py:616
  81.2 0.6 last.1
  81.8 20.4 %all_to_all.82.grams_ref = f32[128,2,128]{2,1,0:T(2,128)S(1)} all-to-all(f32[128,2,128]{2,1,0:T(2,128)S(1)} %get-tuple-element.188), channel_id=1, replica_groups=mesh['grp_0'=4,'grp_1'=2,'rep_0'=4,'rep_1'=4] {'grp_0','grp_1','rep_0','..., dimensions={0} | all-to-all | bytes 262144 | tf_op jit(solution)/shard_map/all_to_all | solution.py:623
  102.2 1.3 %finish.1 = f32[32,128]{1,0:T(8,128)} custom-call(f32[128,2,128]{2,1,0:T(2,128)S(1)} %all_to_all.82.grams_ref, f32[32,128]{1,0:T(8,128)S(1)} %get-tuple-element.189.cur_ref), custom_call_target="tpu_custom_call" | custom-call | tf_op jit(solution)/shard_map/finish/pallas_call | solution.py:624
Async XLA Ops:
  3.7 14.8 %all-to-all-start.12 = ((f32[16,1,128]{2,1,0:T(1,128)}), f32[16,1,128]{2,1,0:T(1,128)S(1)}, u32[]{:S(2)}, u32[]{:S(2)}) async-start(f32[16,1,128]{2,1,0:T(1,128)} %get-tuple-element.171), calls=%async_computation.12 | async-start | bytes 16384 | tf_op jit(solution)/shard_map/all_to_all | solution.py:565
  12.2 6.4 %copy-start.1 = (s32[16]{0:T(128)S(1)}, s32[16]{0:T(128)}, u32[]{:S(2)}) copy-start(s32[16]{0:T(128)} %trunc_ref.3) | copy-start | bytes 196
  18.5 41.0 %copy-start = (s32[50,128]{1,0:T(8,128)S(1)}, s32[50,128]{1,0:T(8,128)}, u32[]{:S(2)}) copy-start(s32[50,128]{1,0:T(8,128)} %nb_ref.1) | copy-start | bytes 76804
where the time goes:
time: 106 us; the launch traced here: 104 us
  blocking collectives  76.1 us (72%)
  Pallas kernels  15.8 us (15%)
  starting transfers between devices  8.43 us (8%)
  waiting for transfers between devices  1.59 us (2%)
  between operations  1.35 us (1%)
    all_to_all x1, blocking collectives, exchange(): received = lax.all_to_all(sent, REP, 0, 0, tiled=True)  36.3 us
    all_to_all x1, blocking collectives, shards(): grams = lax.all_to_all(gram, GRP_REP, 0, 0, tiled=True)  20.4 us
    all_to_all x2, blocking collectives, shards(): columns = lax.all_to_all(columns, REP, 0, 0, tiled=True)  19.4 us
    all_to_all x1, starting transfers between devices, shards(): asked = lax.all_to_all(requests, REP, 0, 0, tiled=True)  8.43 us
    pallas_call x1, Pallas kernels, shards(): pl.pallas_call(local_kernel, out_shape=(struct((HEAD + FULL, 2 * PD), BF1...  4.1 us
    pallas_call x1, Pallas kernels, shards(): pl.pallas_call(slot_kernel, out_shape=(struct((1,), jnp.int32), struct((N...  3.09 us
    pallas_call x1, Pallas kernels, exchange(): pl.pallas_call(functools.partial(far_kernel, size), out_shape=(struct((PA...  3.09 us
  transfers between devices with their start and end apart: 1, of which 1 were waited for; matrix products, arithmetic and copies ran while one was open for 0% of the time, Pallas kernels for 4%

commit v1 on v0

--- a/solution.py
+++ b/solution.py
@@ -17,12 +17,15 @@
 CAP = 64
 CW = 2048
 FULL = RAD * ANG
-SIZES = (384, 512, 544, 576, 608, 640, 672, 704, 736, 768, 896, FULL)
+SIZES = (
+    384, 512, 544, 576, 592, 608, 624, 640, 656, 672, 688, 704, 736, 768, 896, FULL
+)
 HEAD = 2 * VEC
 PEERS = 16
 PAIRS = PEERS // 2
 WIDE = 4
 GROUP = 8
+ALWAYS = 16
 GRP = ("grp_0", "grp_1")
 REP = ("rep_0", "rep_1")
 GRP_REP = ("grp_0", "grp_1", "rep_0", "rep_1")
@@ -121,31 +124,29 @@
         rank = jnp.where(owner == p, here, rank)
     rank = rank.astype(jnp.int32)
     code = jnp.where(remote, owner * CAP + rank, -1)
-    pair = code >> 7
-    lane = jnp.where(remote, code & (PD - 1), -1)
+    place_in_list = jnp.where(remote, rank, -1)
     particle = iota((1, PD), 1).astype(F32) + 1.0
-    rows8 = iota((PAIRS, PD), 0)
-    rows128 = iota((PD, PD), 0)
+    peer = iota((PEERS, PD), 0)
+    target = iota((CAP, PD), 0)
     for n in range(NB):
-        mine = rows8 == pair[n : n + 1, :]
+        mine = peer == owner[n : n + 1, :]
         names = within[n : n + 1, :].astype(F32)
         both = jnp.concatenate(
             [jnp.where(mine, names, 0.0), jnp.where(mine, particle, 0.0)], axis=0
         )
         a_ref[:, n * PD : (n + 1) * PD] = both.astype(BF16)
-        b_ref[:, n * PD : (n + 1) * PD] = one_hot(rows128 == lane[n : n + 1, :])
+        b_ref[:, n * PD : (n + 1) * PD] = one_hot(target == place_in_list[n : n + 1, :])
     lists = lax.dot_general(a_ref[...], b_ref[...], NT, preferred_element_type=F32)
-    turned = pltpu.roll(lists, CAP, 1)
-    first = iota((2 * PAIRS, PD), 1) < CAP
-    both = (jnp.where(first, lists, turned), jnp.where(first, turned, lists))
+    lists = jnp.concatenate([lists, lists], axis=1)
     for p in range(PEERS):
-        r = p // 2
-        req_ref[p] = both[p % 2][r : r + 1, :]
-    lists_ref[...] = lists[PAIRS:]
+        req_ref[p] = lists[p : p + 1, :]
+    names_ref[...] = lists[PEERS:]
+    first = iota((1, PD), 1) < CAP
+    for r in range(PAIRS):
+        even = lists[PEERS + 2 * r : PEERS + 2 * r + 1, :]
+        odd = lists[PEERS + 2 * r + 1 : PEERS + 2 * r + 2, :]
+        lists_ref[r : r + 1, :] = jnp.where(first, even, odd)
     code_ref[...] = code
-    for p in range(PEERS):
-        r = p // 2
-        names_ref[p : p + 1, :] = both[p % 2][PAIRS + r : PAIRS + r + 1, :]
     for copy in bring:
         copy.wait()
 
@@ -239,7 +240,7 @@
     for first in range(0, ANG, GROUP):
         for k in range(first, first + GROUP):
             rows = xt_ref[pl.ds(k, 2 * RAD, stride=ANG), :]
-            masked = rows if k < 16 else jnp.where(kept > k, rows, 0.0)
+            masked = rows if k < ALWAYS else jnp.where(kept > k, rows, 0.0)
             turned = jnp.concatenate([masked[RAD:], -masked[:RAD]], axis=0)
             right = jnp.concatenate([masked, turned], axis=1).astype(BF16)
             s_ref[k] = lax.dot_general(
@@ -301,10 +302,14 @@
     offset = 0
     for q in range(RAD):
         here = pl.ds(offset, ANG)
-        inside = freq < trunc_ref[q]
+        inside = freq[ALWAYS:] < trunc_ref[q]
         for b in range(WIDE // 2):
             for v, ref in enumerate((same_ref, cross_ref)):
-                totals[b][v] = totals[b][v] + jnp.where(inside, ref[b, here, :], 0.0)
+                window = ref[b, here, :]
+                window = jnp.concatenate(
+                    [window[:ALWAYS], jnp.where(inside, window[ALWAYS:], 0.0)], axis=0
+                )
+                totals[b][v] = totals[b][v] + window
         offset = offset + trunc_ref[q]
     inner = (freq > 0) & (freq < ANG - 1)
     for b in range(WIDE // 2):
@@ -550,8 +555,8 @@
         scratch_shapes=[
             pltpu.VMEM((NB, PD), jnp.int32),
             pltpu.VMEM((NBP, PD), jnp.int32),
-            pltpu.VMEM((2 * PAIRS, NB * PD), BF16),
-            pltpu.VMEM((PD, NB * PD), BF16),
+            pltpu.VMEM((2 * PEERS, NB * PD), BF16),
+            pltpu.VMEM((CAP, NB * PD), BF16),
             pltpu.SemaphoreType.DMA((3,)),
         ],
         name="slots",

time: 106 us -> 106 us (level); the launches traced: 104 us -> 108 us
  blocking collectives: 76.1 us -> 80.7 us
    all_to_all x1, blocking collectives: 36.3 us -> 40.7 us  [exchange(): received = lax.all_to_all(sent, REP, 0, 0, tiled=True)]
where the time goes in v1:
time: 106 us; the launch traced here: 108 us
  blocking collectives  80.7 us (76%)
  Pallas kernels  16 us (15%)
  starting transfers between devices  8.43 us (8%)
  waiting for transfers between devices  1.6 us (2%)
  between operations  1.35 us (1%)
    all_to_all x1, blocking collectives, exchange(): received = lax.all_to_all(sent, REP, 0, 0, tiled=True)  40.7 us
    all_to_all x1, blocking collectives, shards(): grams = lax.all_to_all(gram, GRP_REP, 0, 0, tiled=True)  20.4 us
    all_to_all x2, blocking collectives, shards(): columns = lax.all_to_all(columns, REP, 0, 0, tiled=True)  19.5 us
    all_to_all x1, starting transfers between devices, shards(): asked = lax.all_to_all(requests, REP, 0, 0, tiled=True)  8.43 us
    pallas_call x1, Pallas kernels, shards(): pl.pallas_call(local_kernel, out_shape=(struct((HEAD + FULL, 2 * PD), BF1...  4.09 us
    pallas_call x1, Pallas kernels, exchange(): pl.pallas_call(functools.partial(far_kernel, size), out_shape=(struct((PA...  3.28 us
    pallas_call x1, Pallas kernels, shards(): pl.pallas_call(slot_kernel, out_shape=(struct((1,), jnp.int32), struct((N...  2.98 us
  transfers between devices with their start and end apart: 1, of which 1 were waited for; matrix products, arithmetic and copies ran while one was open for 0% of the time, Pallas kernels for 4%

profile of v1, /device:TPU:1, one launch (start us, length us, event | category | flops | bytes accessed | tf_op | source)
XLA Modules:
  0.0 108.1 jit_solution(10161189289122711076)
XLA Ops:
  0.6 3.0 %slots.1 = (s32[1]{0:T(128)}, s32[56,128]{1,0:T(8,128)S(1)}, f32[8,128]{1,0:T(8,128)S(1)}, f32[16,128]{1,0:T(8,128)S(1)}, f32[16,1,128]{2,1,0:T(1,128)}, /*index...) custom-call(s32[16]{0:T(128)} %trunc_ref.3, s32[50,128]{1,0:T(8,128)} %nb_ref.1, bf16[128,2048]{1,0:T(8,128)(2,1)} %coef_hbm.1, ...), custom_call_target="tpu_custom_call" | custom-call | tf_op jit(solution)/shard_map/slots/pallas_call | solution.py:541
  3.6 8.4 %all-to-all-start.16 = ((f32[16,1,128]{2,1,0:T(1,128)}), f32[16,1,128]{2,1,0:T(1,128)S(1)}, u32[]{:S(2)}, u32[]{:S(2)}) async-start(f32[16,1,128]{2,1,0:T(1,128)} %get-tuple-element.219), calls=%async_computation.16 | async-start | bytes 16384 | tf_op jit(solution)/shard_map/all_to_all | solution.py:570
  12.1 0.0 copy-start.1
  12.1 4.1 %local.1 = (bf16[1056,256]{1,0:T(8,128)(2,1)S(1)}, f32[128,128]{1,0:T(8,128)S(1)}, f32[128,128]{1,0:T(8,128)S(1)}, f32[128,128]{1,0:T(8,128)S(1)}) custom-call(s32[16]{0:T(128)} %trunc_ref.3, bf16[128,2048]{1,0:T(8,128)(2,1)S(1)} %get-tuple-element.220.coef_ref, f32[32,128]{1,0:T(8,128)S(1)} %get-tuple-element.221.init_ref), custom_call_target="tpu_custom_call" | custom-call | flops 20000000000 | bytes 1000000 | tf_op jit(solution)/shard_map/local/pallas_call | solution.py:571
  16.8 1.6 %all-to-all-done.16.rx_ref = f32[16,1,128]{2,1,0:T(1,128)S(1)} async-done(((f32[16,1,128]{2,1,0:T(1,128)}), f32[16,1,128]{2,1,0:T(1,128)S(1)}, u32[]{:S(2)}, u32[]{:S(2)}) %all-to-all-start.16) | async-done | bytes 8224 | tf_op jit(solution)/shard_map/all_to_all | solution.py:570
  18.4 0.0 copy-done.1
  18.4 0.0 copy-start
  18.4 45.5 %conditional.1 = ((f32[8,8,128]{2,1,0:T(8,128)S(1)}, f32[16,16,128]{2,1,0:T(8,128)S(1)})) conditional(s32[]{:T(128)} %bitcast, (f32[16,1,128]{2,1,0:T(1,128)S(1)}, bf16[1056,256]{1,0:T(8,128)(2,1)S(1)}, s32[16]{0:T(128)S(1)}, f32[16,128]{1,0:T(8,128)S(1)}) %tuple.90, (f32[16,1,128]{2,1,0:T(1,128)S(1)}, ...), branch_computations={%region_0.0_spmd, %region_1.0_spmd, %region_2.0_spmd, %region_3.0_... | conditional | bytes 8650760 | solution.py:587
  18.4 1.5 %pick.25 = bf16[16,704,128]{2,1,0:T(8,128)(2,1)S(1)} custom-call(f32[16,1,128]{2,1,0:T(1,128)S(1)} %get-tuple-element.167.rx_ref, bf16[1056,256]{1,0:T(8,128)(2,1)S(1)} %get-tuple-element.166.pack_ref), custom_call_target="tpu_custom_call" | custom-call | tf_op jit(solution)/shard_map/cond/branch_9_fun/pick/pallas_call | solution.py:514
  19.9 40.7 %all_to_all.93.recv_ref = bf16[16,704,128]{2,1,0:T(8,128)(2,1)S(1)} all-to-all(bf16[16,704,128]{2,1,0:T(8,128)(2,1)S(1)} %pick.25), channel_id=1, replica_groups=mesh['grp_0'=4,'grp_1'=2,'rep_0'=4,'rep_1'=4] {'rep_0','rep_1'}, dimensions={0} | all-to-all | bytes 5767168 | tf_op jit(solution)/shard_map/cond/branch_9_fun/all_to_all | solution.py:522
  60.6 3.3 %far.25 = (f32[8,8,128]{2,1,0:T(8,128)S(1)}, f32[16,16,128]{2,1,0:T(8,128)S(1)}) custom-call(s32[16]{0:T(128)S(1)} %get-tuple-element.164.trunc_ref, f32[16,128]{1,0:T(8,128)S(1)} %get-tuple-element.165.names_ref, bf16[1056,256]{1,0:T(8,128)(2,1)S(1)} %get-tuple-element.166.pack_ref, bf16[16,704,128]{2,1,0:T(8,128)(2,1)S(1)} %all_to_all.93.recv_ref), custom_call_target="tpu_custom_call" | custom-call | tf_op jit(solution)/shard_map/cond/branch_9_fun/far/pallas_call | solution.py:523
  63.9 0.0 copy-done
  63.9 1.7 %first.1 = (f32[50,2,128]{2,1,0:T(2,128)}, f32[2,128,128]{2,1,0:T(8,128)S(1)}, f32[8,128]{1,0:T(8,128)S(1)}, f32[32,128]{1,0:T(8,128)S(1)}, f32[16,16,128]{2,1,0:T(8,128)S(1)}) custom-call(s32[50,128]{1,0:T(8,128)S(1)} %copy-done, s32[56,128]{1,0:T(8,128)S(1)} %get-tuple-element.216.code_ref, f32[8,128]{1,0:T(8,128)S(1)} %get-tuple-element.217.lists_ref, ...), custom_call_target="tpu_custom_call" | custom-call | tf_op jit(solution)/shard_map/first/pallas_call | solution.py:592
  65.7 9.6 %all_to_all.100.recv_ref = f32[16,16,128]{2,1,0:T(8,128)S(1)} all-to-all(f32[16,16,128]{2,1,0:T(8,128)S(1)} %get-tuple-element.230), channel_id=1, replica_groups=mesh['grp_0'=4,'grp_1'=2,'rep_0'=4,'rep_1'=4] {'rep_0','rep_1'}, dimensions={0} | all-to-all | bytes 262144 | tf_op jit(solution)/shard_map/all_to_all | solution.py:614
  75.2 0.6 middle.1
  75.8 9.9 %all_to_all.101.recv_ref = f32[16,16,128]{2,1,0:T(8,128)S(1)} all-to-all(f32[16,16,128]{2,1,0:T(8,128)S(1)} %get-tuple-element.234), channel_id=1, replica_groups=mesh['grp_0'=4,'grp_1'=2,'rep_0'=4,'rep_1'=4] {'rep_0','rep_1'}, dimensions={0} | all-to-all | bytes 262144 | tf_op jit(solution)/shard_map/all_to_all | solution.py:621
  85.7 0.6 last.1
  86.3 20.4 %all_to_all.102.grams_ref = f32[128,2,128]{2,1,0:T(2,128)S(1)} all-to-all(f32[128,2,128]{2,1,0:T(2,128)S(1)} %get-tuple-element.236), channel_id=1, replica_groups=mesh['grp_0'=4,'grp_1'=2,'rep_0'=4,'rep_1'=4] {'grp_0','grp_1','rep_0','..., dimensions={0} | all-to-all | bytes 262144 | tf_op jit(solution)/shard_map/all_to_all | solution.py:628
  106.8 1.3 %finish.1 = f32[32,128]{1,0:T(8,128)} custom-call(f32[128,2,128]{2,1,0:T(2,128)S(1)} %all_to_all.102.grams_ref, f32[32,128]{1,0:T(8,128)S(1)} %get-tuple-element.237.cur_ref), custom_call_target="tpu_custom_call" | custom-call | tf_op jit(solution)/shard_map/finish/pallas_call | solution.py:629
Async XLA Ops:
  3.6 14.8 %all-to-all-start.16 = ((f32[16,1,128]{2,1,0:T(1,128)}), f32[16,1,128]{2,1,0:T(1,128)S(1)}, u32[]{:S(2)}, u32[]{:S(2)}) async-start(f32[16,1,128]{2,1,0:T(1,128)} %get-tuple-element.219), calls=%async_computation.16 | async-start | bytes 16384 | tf_op jit(solution)/shard_map/all_to_all | solution.py:570
  12.1 6.4 %copy-start.1 = (s32[16]{0:T(128)S(1)}, s32[16]{0:T(128)}, u32[]{:S(2)}) copy-start(s32[16]{0:T(128)} %trunc_ref.3) | copy-start | bytes 196
  18.4 45.5 %copy-start = (s32[50,128]{1,0:T(8,128)S(1)}, s32[50,128]{1,0:T(8,128)}, u32[]{:S(2)}) copy-start(s32[50,128]{1,0:T(8,128)} %nb_ref.1) | copy-start | bytes 76804

commit v2 on v1

--- a/solution.py
+++ b/solution.py
@@ -17,9 +17,7 @@
 CAP = 64
 CW = 2048
 FULL = RAD * ANG
-SIZES = (
-    384, 512, 544, 576, 592, 608, 624, 640, 656, 672, 688, 704, 736, 768, 896, FULL
-)
+SIZES = (384, 512, 544, 576, 608, 640, 672, 704, 736, 768, 896, FULL)
 HEAD = 2 * VEC
 PEERS = 16
 PAIRS = PEERS // 2

time: 106 us -> 107 us (level)
  no operation moved by 1% of the time
where the time goes in v2:
time: 107 us; the launch traced here: 108 us
  blocking collectives  80.5 us (75%)
  Pallas kernels  16 us (15%)
  starting transfers between devices  8.43 us (8%)
  waiting for transfers between devices  1.6 us (1%)
  between operations  1.35 us (1%)
    all_to_all x1, blocking collectives, exchange(): received = lax.all_to_all(sent, REP, 0, 0, tiled=True)  40.3 us
    all_to_all x1, blocking collectives, shards(): grams = lax.all_to_all(gram, GRP_REP, 0, 0, tiled=True)  20.8 us
    all_to_all x2, blocking collectives, shards(): columns = lax.all_to_all(columns, REP, 0, 0, tiled=True)  19.4 us
    all_to_all x1, starting transfers between devices, shards(): asked = lax.all_to_all(requests, REP, 0, 0, tiled=True)  8.43 us
    pallas_call x1, Pallas kernels, shards(): pl.pallas_call(local_kernel, out_shape=(struct((HEAD + FULL, 2 * PD), BF1...  4.09 us
    pallas_call x1, Pallas kernels, exchange(): pl.pallas_call(functools.partial(far_kernel, size), out_shape=(struct((PA...  3.27 us
    pallas_call x1, Pallas kernels, shards(): pl.pallas_call(slot_kernel, out_shape=(struct((1,), jnp.int32), struct((N...  2.98 us
  transfers between devices with their start and end apart: 1, of which 1 were waited for; matrix products, arithmetic and copies ran while one was open for 0% of the time, Pallas kernels for 4%

profile of v2, /device:TPU:1, one launch (start us, length us, event | category | flops | bytes accessed | tf_op | source)
XLA Modules:
  0.0 108.3 jit_solution(4750722258794119510)
XLA Ops:
  0.6 3.0 %slots.1 = (s32[1]{0:T(128)}, s32[56,128]{1,0:T(8,128)S(1)}, f32[8,128]{1,0:T(8,128)S(1)}, f32[16,128]{1,0:T(8,128)S(1)}, f32[16,1,128]{2,1,0:T(1,128)}, /*index...) custom-call(s32[16]{0:T(128)} %trunc_ref.3, s32[50,128]{1,0:T(8,128)} %nb_ref.1, bf16[128,2048]{1,0:T(8,128)(2,1)} %coef_hbm.1, ...), custom_call_target="tpu_custom_call" | custom-call | tf_op jit(solution)/shard_map/slots/pallas_call | solution.py:539
  3.6 8.4 %all-to-all-start.12 = ((f32[16,1,128]{2,1,0:T(1,128)}), f32[16,1,128]{2,1,0:T(1,128)S(1)}, u32[]{:S(2)}, u32[]{:S(2)}) async-start(f32[16,1,128]{2,1,0:T(1,128)} %get-tuple-element.171), calls=%async_computation.12 | async-start | bytes 16384 | tf_op jit(solution)/shard_map/all_to_all | solution.py:568
  12.1 0.0 copy-start.1
  12.1 4.1 %local.1 = (bf16[1056,256]{1,0:T(8,128)(2,1)S(1)}, f32[128,128]{1,0:T(8,128)S(1)}, f32[128,128]{1,0:T(8,128)S(1)}, f32[128,128]{1,0:T(8,128)S(1)}) custom-call(s32[16]{0:T(128)} %trunc_ref.3, bf16[128,2048]{1,0:T(8,128)(2,1)S(1)} %get-tuple-element.172.coef_ref, f32[32,128]{1,0:T(8,128)S(1)} %get-tuple-element.173.init_ref), custom_call_target="tpu_custom_call" | custom-call | flops 20000000000 | bytes 1000000 | tf_op jit(solution)/shard_map/local/pallas_call | solution.py:569
  16.8 1.6 %all-to-all-done.12.rx_ref = f32[16,1,128]{2,1,0:T(1,128)S(1)} async-done(((f32[16,1,128]{2,1,0:T(1,128)}), f32[16,1,128]{2,1,0:T(1,128)S(1)}, u32[]{:S(2)}, u32[]{:S(2)}) %all-to-all-start.12) | async-done | bytes 8224 | tf_op jit(solution)/shard_map/all_to_all | solution.py:568
  18.4 0.0 copy-done.1
  18.4 0.0 copy-start
  18.4 45.4 %conditional.1 = ((f32[8,8,128]{2,1,0:T(8,128)S(1)}, f32[16,16,128]{2,1,0:T(8,128)S(1)})) conditional(s32[]{:T(128)} %bitcast, (f32[16,1,128]{2,1,0:T(1,128)S(1)}, bf16[1056,256]{1,0:T(8,128)(2,1)S(1)}, s32[16]{0:T(128)S(1)}, f32[16,128]{1,0:T(8,128)S(1)}) %tuple.70, (f32[16,1,128]{2,1,0:T(1,128)S(1)}, ...), branch_computations={%region_0.0_spmd, %region_1.0_spmd, %region_2.0_spmd, %region_3.0_... | conditional | bytes 8650760 | solution.py:585
  18.4 1.5 %pick.18 = bf16[16,704,128]{2,1,0:T(8,128)(2,1)S(1)} custom-call(f32[16,1,128]{2,1,0:T(1,128)S(1)} %get-tuple-element.123.rx_ref, bf16[1056,256]{1,0:T(8,128)(2,1)S(1)} %get-tuple-element.122.pack_ref), custom_call_target="tpu_custom_call" | custom-call | tf_op jit(solution)/shard_map/cond/branch_6_fun/pick/pallas_call | solution.py:512
  19.9 40.3 %all_to_all.74.recv_ref = bf16[16,704,128]{2,1,0:T(8,128)(2,1)S(1)} all-to-all(bf16[16,704,128]{2,1,0:T(8,128)(2,1)S(1)} %pick.18), channel_id=1, replica_groups=mesh['grp_0'=4,'grp_1'=2,'rep_0'=4,'rep_1'=4] {'rep_0','rep_1'}, dimensions={0} | all-to-all | bytes 5767168 | tf_op jit(solution)/shard_map/cond/branch_6_fun/all_to_all | solution.py:520
  60.1 3.3 %far.18 = (f32[8,8,128]{2,1,0:T(8,128)S(1)}, f32[16,16,128]{2,1,0:T(8,128)S(1)}) custom-call(s32[16]{0:T(128)S(1)} %get-tuple-element.120.trunc_ref, f32[16,128]{1,0:T(8,128)S(1)} %get-tuple-element.121.names_ref, bf16[1056,256]{1,0:T(8,128)(2,1)S(1)} %get-tuple-element.122.pack_ref, bf16[16,704,128]{2,1,0:T(8,128)(2,1)S(1)} %all_to_all.74.recv_ref), custom_call_target="tpu_custom_call" | custom-call | tf_op jit(solution)/shard_map/cond/branch_6_fun/far/pallas_call | solution.py:521
  63.8 0.0 copy-done
  63.8 1.7 %first.1 = (f32[50,2,128]{2,1,0:T(2,128)}, f32[2,128,128]{2,1,0:T(8,128)S(1)}, f32[8,128]{1,0:T(8,128)S(1)}, f32[32,128]{1,0:T(8,128)S(1)}, f32[16,16,128]{2,1,0:T(8,128)S(1)}) custom-call(s32[50,128]{1,0:T(8,128)S(1)} %copy-done, s32[56,128]{1,0:T(8,128)S(1)} %get-tuple-element.168.code_ref, f32[8,128]{1,0:T(8,128)S(1)} %get-tuple-element.169.lists_ref, ...), custom_call_target="tpu_custom_call" | custom-call | tf_op jit(solution)/shard_map/first/pallas_call | solution.py:590
  65.6 9.8 %all_to_all.80.recv_ref = f32[16,16,128]{2,1,0:T(8,128)S(1)} all-to-all(f32[16,16,128]{2,1,0:T(8,128)S(1)} %get-tuple-element.182), channel_id=1, replica_groups=mesh['grp_0'=4,'grp_1'=2,'rep_0'=4,'rep_1'=4] {'rep_0','rep_1'}, dimensions={0} | all-to-all | bytes 262144 | tf_op jit(solution)/shard_map/all_to_all | solution.py:612
  75.4 0.6 middle.1
  76.0 9.6 %all_to_all.81.recv_ref = f32[16,16,128]{2,1,0:T(8,128)S(1)} all-to-all(f32[16,16,128]{2,1,0:T(8,128)S(1)} %get-tuple-element.186), channel_id=1, replica_groups=mesh['grp_0'=4,'grp_1'=2,'rep_0'=4,'rep_1'=4] {'rep_0','rep_1'}, dimensions={0} | all-to-all | bytes 262144 | tf_op jit(solution)/shard_map/all_to_all | solution.py:619
  85.6 0.6 last.1
  86.2 20.8 %all_to_all.82.grams_ref = f32[128,2,128]{2,1,0:T(2,128)S(1)} all-to-all(f32[128,2,128]{2,1,0:T(2,128)S(1)} %get-tuple-element.188), channel_id=1, replica_groups=mesh['grp_0'=4,'grp_1'=2,'rep_0'=4,'rep_1'=4] {'grp_0','grp_1','rep_0','..., dimensions={0} | all-to-all | bytes 262144 | tf_op jit(solution)/shard_map/all_to_all | solution.py:626
  107.0 1.3 %finish.1 = f32[32,128]{1,0:T(8,128)} custom-call(f32[128,2,128]{2,1,0:T(2,128)S(1)} %all_to_all.82.grams_ref, f32[32,128]{1,0:T(8,128)S(1)} %get-tuple-element.189.cur_ref), custom_call_target="tpu_custom_call" | custom-call | tf_op jit(solution)/shard_map/finish/pallas_call | solution.py:627
Async XLA Ops:
  3.6 14.8 %all-to-all-start.12 = ((f32[16,1,128]{2,1,0:T(1,128)}), f32[16,1,128]{2,1,0:T(1,128)S(1)}, u32[]{:S(2)}, u32[]{:S(2)}) async-start(f32[16,1,128]{2,1,0:T(1,128)} %get-tuple-element.171), calls=%async_computation.12 | async-start | bytes 16384 | tf_op jit(solution)/shard_map/all_to_all | solution.py:568
  12.1 6.4 %copy-start.1 = (s32[16]{0:T(128)S(1)}, s32[16]{0:T(128)}, u32[]{:S(2)}) copy-start(s32[16]{0:T(128)} %trunc_ref.3) | copy-start | bytes 196
  18.4 45.4 %copy-start = (s32[50,128]{1,0:T(8,128)S(1)}, s32[50,128]{1,0:T(8,128)}, u32[]{:S(2)}) copy-start(s32[50,128]{1,0:T(8,128)} %nb_ref.1) | copy-start | bytes 76804

commit v3 on v2

--- a/solution.py
+++ b/solution.py
@@ -22,7 +22,7 @@
 PEERS = 16
 PAIRS = PEERS // 2
 WIDE = 4
-GROUP = 8
+GROUP = 4
 ALWAYS = 16
 GRP = ("grp_0", "grp_1")
 REP = ("rep_0", "rep_1")

time: 107 us -> 104 us (0.972); the launches traced: 108 us -> 103 us
  blocking collectives: 80.5 us -> 76.1 us
    all_to_all x1, blocking collectives: 40.3 us -> 36.4 us  [exchange(): received = lax.all_to_all(sent, REP, 0, 0, tiled=True)]
where the time goes in v3:
time: 104 us; the launch traced here: 103 us
  blocking collectives  76.1 us (73%)
  Pallas kernels  15.7 us (15%)
  starting transfers between devices  8.43 us (8%)
  waiting for transfers between devices  1.56 us (2%)
  between operations  1.35 us (1%)
    all_to_all x1, blocking collectives, exchange(): received = lax.all_to_all(sent, REP, 0, 0, tiled=True)  36.4 us
    all_to_all x1, blocking collectives, shards(): grams = lax.all_to_all(gram, GRP_REP, 0, 0, tiled=True)  20.4 us
    all_to_all x2, blocking collectives, shards(): columns = lax.all_to_all(columns, REP, 0, 0, tiled=True)  19.4 us
    all_to_all x1, starting transfers between devices, shards(): asked = lax.all_to_all(requests, REP, 0, 0, tiled=True)  8.43 us
    pallas_call x1, Pallas kernels, shards(): pl.pallas_call(local_kernel, out_shape=(struct((HEAD + FULL, 2 * PD), BF1...  4.12 us
    pallas_call x1, Pallas kernels, exchange(): pl.pallas_call(functools.partial(far_kernel, size), out_shape=(struct((PA...  3.03 us
    pallas_call x1, Pallas kernels, shards(): pl.pallas_call(slot_kernel, out_shape=(struct((1,), jnp.int32), struct((N...  2.98 us
  transfers between devices with their start and end apart: 1, of which 1 were waited for; matrix products, arithmetic and copies ran while one was open for 0% of the time, Pallas kernels for 4%

profile of v3, /device:TPU:1, one launch (start us, length us, event | category | flops | bytes accessed | tf_op | source)
XLA Modules:
  0.0 103.4 jit_solution(7514935884720752169)
XLA Ops:
  0.6 3.0 %slots.1 = (s32[1]{0:T(128)}, s32[56,128]{1,0:T(8,128)S(1)}, f32[8,128]{1,0:T(8,128)S(1)}, f32[16,128]{1,0:T(8,128)S(1)}, f32[16,1,128]{2,1,0:T(1,128)}, /*index...) custom-call(s32[16]{0:T(128)} %trunc_ref.3, s32[50,128]{1,0:T(8,128)} %nb_ref.1, bf16[128,2048]{1,0:T(8,128)(2,1)} %coef_hbm.1, ...), custom_call_target="tpu_custom_call" | custom-call | tf_op jit(solution)/shard_map/slots/pallas_call | solution.py:539
  3.6 8.4 %all-to-all-start.12 = ((f32[16,1,128]{2,1,0:T(1,128)}), f32[16,1,128]{2,1,0:T(1,128)S(1)}, u32[]{:S(2)}, u32[]{:S(2)}) async-start(f32[16,1,128]{2,1,0:T(1,128)} %get-tuple-element.171), calls=%async_computation.12 | async-start | bytes 16384 | tf_op jit(solution)/shard_map/all_to_all | solution.py:568
  12.1 0.0 copy-start.1
  12.1 4.1 %local.1 = (bf16[1056,256]{1,0:T(8,128)(2,1)S(1)}, f32[128,128]{1,0:T(8,128)S(1)}, f32[128,128]{1,0:T(8,128)S(1)}, f32[128,128]{1,0:T(8,128)S(1)}) custom-call(s32[16]{0:T(128)} %trunc_ref.3, bf16[128,2048]{1,0:T(8,128)(2,1)S(1)} %get-tuple-element.172.coef_ref, f32[32,128]{1,0:T(8,128)S(1)} %get-tuple-element.173.init_ref), custom_call_target="tpu_custom_call" | custom-call | flops 20000000000 | bytes 1000000 | tf_op jit(solution)/shard_map/local/pallas_call | solution.py:569
  16.9 1.6 %all-to-all-done.12.rx_ref = f32[16,1,128]{2,1,0:T(1,128)S(1)} async-done(((f32[16,1,128]{2,1,0:T(1,128)}), f32[16,1,128]{2,1,0:T(1,128)S(1)}, u32[]{:S(2)}, u32[]{:S(2)}) %all-to-all-start.12) | async-done | bytes 8224 | tf_op jit(solution)/shard_map/all_to_all | solution.py:568
  18.4 0.0 copy-done.1
  18.4 0.0 copy-start
  18.4 41.0 %conditional.1 = ((f32[8,8,128]{2,1,0:T(8,128)S(1)}, f32[16,16,128]{2,1,0:T(8,128)S(1)})) conditional(s32[]{:T(128)} %bitcast, (f32[16,1,128]{2,1,0:T(1,128)S(1)}, bf16[1056,256]{1,0:T(8,128)(2,1)S(1)}, s32[16]{0:T(128)S(1)}, f32[16,128]{1,0:T(8,128)S(1)}) %tuple.70, (f32[16,1,128]{2,1,0:T(1,128)S(1)}, ...), branch_computations={%region_0.0_spmd, %region_1.0_spmd, %region_2.0_spmd, %region_3.0_... | conditional | bytes 8650760 | solution.py:585
  18.4 1.4 %pick.15 = bf16[16,608,128]{2,1,0:T(8,128)(2,1)S(1)} custom-call(f32[16,1,128]{2,1,0:T(1,128)S(1)} %get-tuple-element.111.rx_ref, bf16[1056,256]{1,0:T(8,128)(2,1)S(1)} %get-tuple-element.110.pack_ref), custom_call_target="tpu_custom_call" | custom-call | tf_op jit(solution)/shard_map/cond/branch_3_fun/pick/pallas_call | solution.py:512
  19.8 36.4 %all_to_all.71.recv_ref = bf16[16,608,128]{2,1,0:T(8,128)(2,1)S(1)} all-to-all(bf16[16,608,128]{2,1,0:T(8,128)(2,1)S(1)} %pick.15), channel_id=1, replica_groups=mesh['grp_0'=4,'grp_1'=2,'rep_0'=4,'rep_1'=4] {'rep_0','rep_1'}, dimensions={0} | all-to-all | bytes 4980736 | tf_op jit(solution)/shard_map/cond/branch_3_fun/all_to_all | solution.py:520
  56.1 3.0 %far.15 = (f32[8,8,128]{2,1,0:T(8,128)S(1)}, f32[16,16,128]{2,1,0:T(8,128)S(1)}) custom-call(s32[16]{0:T(128)S(1)} %get-tuple-element.108.trunc_ref, f32[16,128]{1,0:T(8,128)S(1)} %get-tuple-element.109.names_ref, bf16[1056,256]{1,0:T(8,128)(2,1)S(1)} %get-tuple-element.110.pack_ref, bf16[16,608,128]{2,1,0:T(8,128)(2,1)S(1)} %all_to_all.71.recv_ref), custom_call_target="tpu_custom_call" | custom-call | tf_op jit(solution)/shard_map/cond/branch_3_fun/far/pallas_call | solution.py:521
  59.4 0.0 copy-done
  59.4 1.7 %first.1 = (f32[50,2,128]{2,1,0:T(2,128)}, f32[2,128,128]{2,1,0:T(8,128)S(1)}, f32[8,128]{1,0:T(8,128)S(1)}, f32[32,128]{1,0:T(8,128)S(1)}, f32[16,16,128]{2,1,0:T(8,128)S(1)}) custom-call(s32[50,128]{1,0:T(8,128)S(1)} %copy-done, s32[56,128]{1,0:T(8,128)S(1)} %get-tuple-element.168.code_ref, f32[8,128]{1,0:T(8,128)S(1)} %get-tuple-element.169.lists_ref, ...), custom_call_target="tpu_custom_call" | custom-call | tf_op jit(solution)/shard_map/first/pallas_call | solution.py:590
  61.2 9.5 %all_to_all.80.recv_ref = f32[16,16,128]{2,1,0:T(8,128)S(1)} all-to-all(f32[16,16,128]{2,1,0:T(8,128)S(1)} %get-tuple-element.182), channel_id=1, replica_groups=mesh['grp_0'=4,'grp_1'=2,'rep_0'=4,'rep_1'=4] {'rep_0','rep_1'}, dimensions={0} | all-to-all | bytes 262144 | tf_op jit(solution)/shard_map/all_to_all | solution.py:612
  70.6 0.6 middle.1
  71.2 9.9 %all_to_all.81.recv_ref = f32[16,16,128]{2,1,0:T(8,128)S(1)} all-to-all(f32[16,16,128]{2,1,0:T(8,128)S(1)} %get-tuple-element.186), channel_id=1, replica_groups=mesh['grp_0'=4,'grp_1'=2,'rep_0'=4,'rep_1'=4] {'rep_0','rep_1'}, dimensions={0} | all-to-all | bytes 262144 | tf_op jit(solution)/shard_map/all_to_all | solution.py:619
  81.1 0.6 last.1
  81.7 20.4 %all_to_all.82.grams_ref = f32[128,2,128]{2,1,0:T(2,128)S(1)} all-to-all(f32[128,2,128]{2,1,0:T(2,128)S(1)} %get-tuple-element.188), channel_id=1, replica_groups=mesh['grp_0'=4,'grp_1'=2,'rep_0'=4,'rep_1'=4] {'grp_0','grp_1','rep_0','..., dimensions={0} | all-to-all | bytes 262144 | tf_op jit(solution)/shard_map/all_to_all | solution.py:626
  102.1 1.3 %finish.1 = f32[32,128]{1,0:T(8,128)} custom-call(f32[128,2,128]{2,1,0:T(2,128)S(1)} %all_to_all.82.grams_ref, f32[32,128]{1,0:T(8,128)S(1)} %get-tuple-element.189.cur_ref), custom_call_target="tpu_custom_call" | custom-call | tf_op jit(solution)/shard_map/finish/pallas_call | solution.py:627
Async XLA Ops:
  3.6 14.8 %all-to-all-start.12 = ((f32[16,1,128]{2,1,0:T(1,128)}), f32[16,1,128]{2,1,0:T(1,128)S(1)}, u32[]{:S(2)}, u32[]{:S(2)}) async-start(f32[16,1,128]{2,1,0:T(1,128)} %get-tuple-element.171), calls=%async_computation.12 | async-start | bytes 16384 | tf_op jit(solution)/shard_map/all_to_all | solution.py:568
  12.1 6.4 %copy-start.1 = (s32[16]{0:T(128)S(1)}, s32[16]{0:T(128)}, u32[]{:S(2)}) copy-start(s32[16]{0:T(128)} %trunc_ref.3) | copy-start | bytes 196
  18.4 41.0 %copy-start = (s32[50,128]{1,0:T(8,128)S(1)}, s32[50,128]{1,0:T(8,128)}, u32[]{:S(2)}) copy-start(s32[50,128]{1,0:T(8,128)} %nb_ref.1) | copy-start | bytes 76804
